TPU v7x, 32 devices: a whole 2x2x4 slice. The times are simulated.
32 devices in a mesh: groups: 2 (over x), seq: 16 (over z, y, core).
Axes of the slice: x: 2, y: 2, z: 4, core: 2. Of those that a mesh axis runs over, the one named last changes fastest.
Arguments:
- queries: bfloat16 [4, 2048, 4096], P('groups', 'seq'), parts along dimension 0, may hold values from -120 to 120
- key_states: bfloat16 [4, 2048, 4096], P('groups', 'seq'), parts along dimension 0, may hold values from -4 to 4
- value_states: bfloat16 [4, 2048, 4096], P('groups', 'seq'), parts along dimension 0, may hold values from -6 to 6
- random_blocks: int32 [4, 32, 3], P('groups'), parts along dimension 0, may hold values from 0 to 31
- global_blocks: int32 [4, 2], P('groups'), parts along dimension 0, may hold values from 0 to 31, as said below
Outputs:
- attended: bfloat16 [4, 2048, 4096], P('groups', 'seq'), parts along dimension 0
There are 2 independent parts, one for each index of `groups`. A program takes and returns all parts, laid end to end along the dimension named above; each array names one. Nothing has to cross between parts.
Inputs may be any that keep to these rules, and one draw needn't show every extreme that they name: `global_blocks`: the 2 global blocks of a document are different, the first below 16 and the second not.
All inputs are finite; a program needn't handle non-finite values.
Results may differ from a plain program's by a relative error of at most 0.008.
Values may be sent and summed in bfloat16 or wider, within the bound.
A program may use at most 128 MiB of HBM per device.

v0:
```python
import math

import jax
import jax.numpy as jnp
from jax import lax
from jax.sharding import PartitionSpec as P

HEAD_DIM = 128
BLOCK = 64
NGLOB = 2
NRAND = 3


def from_partner(block, axis, distance):
    count = lax.axis_size(axis)
    route = []
    for low in range(count):
        high = low | 1 << distance
        if high != low and high < count:
            route += [(low, high), (high, low)]
    return lax.ppermute(block, axis, route)


def soft_weights(scores):
    row_max = jnp.max(scores, axis=-1, keepdims=True)
    exponent = jnp.exp(scores - row_max)
    return (exponent / jnp.sum(exponent, axis=-1, keepdims=True)).astype(jnp.bfloat16)


def global_rows(query_rows, key_tokens, value_tokens):
    scores = jnp.einsum(
        "qhs,khs->hqk", query_rows, key_tokens, preferred_element_type=jnp.float32
    ) * HEAD_DIM ** (-0.5)
    weights = soft_weights(scores)
    return jnp.einsum(
        "hqk,khs->qhs", weights, value_tokens, preferred_element_type=jnp.float32
    ).astype(jnp.bfloat16)


def per_device(queries, key_states, value_states, random_blocks, global_blocks):
    devices = lax.axis_size("seq")
    device = lax.axis_index("seq")
    documents = queries.shape[0]
    head_groups = devices // (2 * documents)
    group_width = queries.shape[2] // head_groups
    heads_here = group_width // HEAD_DIM
    block_len = BLOCK
    total_blocks = 2 * devices
    parity = device % 2
    document = device // (2 * head_groups)

    def by_parity(states):
        pieces = states.reshape(documents, 2, block_len, head_groups, group_width)
        return pieces.transpose(0, 3, 1, 2, 4).reshape(devices, block_len, group_width)

    query_recv, key_half, value_half = (
        lax.all_to_all(by_parity(queries), "seq", split_axis=0, concat_axis=1, tiled=True),
        lax.all_to_all(by_parity(key_states), "seq", split_axis=0, concat_axis=1, tiled=True),
        lax.all_to_all(by_parity(value_states), "seq", split_axis=0, concat_axis=1, tiled=True),
    )
    key_other, value_other = from_partner((key_half, value_half), "seq", 0)

    def alternate(own_rows, their_rows):
        own_rows = own_rows.reshape(devices, 1, block_len, group_width)
        their_rows = their_rows.reshape(devices, 1, block_len, group_width)
        joined = jnp.where(
            parity == 0,
            jnp.concatenate([own_rows, their_rows], axis=1),
            jnp.concatenate([their_rows, own_rows], axis=1),
        )
        return joined.reshape(total_blocks * block_len, group_width)

    key_flat = alternate(key_half, key_other)
    value_flat = alternate(value_half, value_other)
    key_blocks = key_flat.reshape(total_blocks, block_len, heads_here, HEAD_DIM)
    value_blocks = value_flat.reshape(total_blocks, block_len, heads_here, HEAD_DIM)
    key_tokens = key_flat.reshape(total_blocks * block_len, heads_here, HEAD_DIM)
    value_tokens = value_flat.reshape(total_blocks * block_len, heads_here, HEAD_DIM)
    query_mine = query_recv.reshape(devices, block_len, heads_here, HEAD_DIM)
    document_lists = lax.dynamic_index_in_dim(random_blocks, document, 0, keepdims=False)
    own_lists = lax.dynamic_index_in_dim(
        document_lists.reshape(devices, 2, NRAND), parity, 1, keepdims=False
    )
    globals_here = lax.dynamic_index_in_dim(global_blocks, document, 0, keepdims=False)
    positions = 2 * jnp.arange(devices, dtype=jnp.int32) + parity
    listed = jnp.concatenate(
        [
            jnp.broadcast_to(globals_here[None, :], (devices, NGLOB)),
            (positions - 1)[:, None],
            positions[:, None],
            (positions + 1)[:, None],
            own_lists,
        ],
        axis=1,
    )
    live_mask = jnp.concatenate(
        [
            jnp.ones((devices, NGLOB), jnp.bool_),
            (positions >= 1)[:, None],
            jnp.ones((devices, 1), jnp.bool_),
            (positions + 1 < total_blocks)[:, None],
            jnp.ones((devices, NRAND), jnp.bool_),
        ],
        axis=1,
    )
    listed = jnp.clip(listed, 0, total_blocks - 1)
    per_step = math.gcd(devices, max(1, 512 // block_len))
    step_count = devices // per_step

    def local_group(packed):
        query_group, listed_group, live_group = packed
        gathered_keys = jnp.take(key_blocks, listed_group, axis=0).reshape(
            per_step, -1, heads_here, HEAD_DIM
        )
        gathered_values = jnp.take(value_blocks, listed_group, axis=0).reshape(
            per_step, -1, heads_here, HEAD_DIM
        )
        scores = jnp.einsum(
            "pqhs,pkhs->phqk", query_group, gathered_keys, preferred_element_type=jnp.float32
        ) * HEAD_DIM ** (-0.5)
        live_tokens = jnp.repeat(live_group, block_len, axis=1)
        scores = jnp.where(live_tokens[:, None, None, :], scores, -1e30)
        weights = soft_weights(scores)
        return jnp.einsum(
            "phqk,pkhs->pqhs", weights, gathered_values, preferred_element_type=jnp.float32
        ).astype(jnp.bfloat16)

    attended = lax.map(
        local_group,
        (
            query_mine.reshape(step_count, per_step, block_len, heads_here, HEAD_DIM),
            listed.reshape(step_count, per_step, -1),
            live_mask.reshape(step_count, per_step, -1),
        ),
    )
    attended = attended.reshape(devices, block_len, heads_here, HEAD_DIM)
    owned = [globals_here[slot_index] % 2 == parity for slot_index in range(NGLOB)]
    places = [globals_here[slot_index] // 2 for slot_index in range(NGLOB)]
    for slot_index in range(NGLOB):
        place_here = places[slot_index]

        def compute_rows(current):
            rows_here = lax.dynamic_index_in_dim(query_mine, place_here, 0, keepdims=False)
            return lax.dynamic_update_index_in_dim(
                current, global_rows(rows_here, key_tokens, value_tokens), place_here, 0
            )

        def keep_rows(current):
            return current

        attended = lax.cond(owned[slot_index], compute_rows, keep_rows, attended)
    returned = lax.all_to_all(
        attended.reshape(devices, block_len, group_width),
        "seq",
        split_axis=0,
        concat_axis=0,
        tiled=True,
    )
    returned = returned.reshape(documents, head_groups, 2, block_len, group_width).transpose(
        0, 2, 3, 1, 4
    )
    return returned.reshape(documents, 2 * block_len, head_groups * group_width)


def solution(mesh):
    placed = (
        P("groups", "seq", None),
        P("groups", "seq", None),
        P("groups", "seq", None),
        P("groups", None, None),
        P("groups", None),
    )
    return jax.shard_map(
        per_device, mesh=mesh, in_specs=placed, out_specs=P("groups", "seq", None), check_vma=False
    )
```

profile of v0, /device:TPU:1, one launch (start us, length us, event | category | flops | bytes accessed | tf_op | source)
XLA Modules:
  0.0 424.9 jit_solution(15134097178231390452)
XLA Ops:
  0.0 3.3 reshape.163
  5.3 7.3 %all-to-all-start = ((bf16[16,64,1024]{2,1,0:T(8,128)(2,1)}), bf16[16,64,1024]{2,1,0:T(8,128)(2,1)}, u32[]{:S(2)}, u32[]{:S(2)}) async-start(bf16[16,64,1024]{2,1,0:T(8,128)(2,1)} %bitcast.19), calls=%async_computation | async-start | bytes 4194304 | tf_op jit(solution)/shard_map/all_to_all | solution.py:59
  12.6 3.3 reshape.168
  17.9 36.3 %all-to-all-done = bf16[16,64,1024]{2,1,0:T(8,128)(2,1)} async-done(((bf16[16,64,1024]{2,1,0:T(8,128)(2,1)}), bf16[16,64,1024]{2,1,0:T(8,128)(2,1)}, u32[]{:S(2)}, u32[]{:S(2)}) %all-to-all-start) | async-done | bytes 2097184 | tf_op jit(solution)/shard_map/all_to_all | solution.py:59
  54.3 10.7 %all-to-all-start.2 = ((bf16[16,64,1024]{2,1,0:T(8,128)(2,1)}), bf16[16,64,1024]{2,1,0:T(8,128)(2,1)}, u32[]{:S(2)}, u32[]{:S(2)}) async-start(bf16[16,64,1024]{2,1,0:T(8,128)(2,1)} %bitcast.26), calls=%async_computation.2 | async-start | bytes 4194304 | tf_op jit(solution)/shard_map/all_to_all | solution.py:58
  64.9 3.3 reshape.166
  70.3 36.3 %all-to-all-done.2 = bf16[16,64,1024]{2,1,0:T(8,128)(2,1)} async-done(((bf16[16,64,1024]{2,1,0:T(8,128)(2,1)}), bf16[16,64,1024]{2,1,0:T(8,128)(2,1)}, u32[]{:S(2)}, u32[]{:S(2)}) %all-to-all-start.2) | async-done | bytes 2097184 | tf_op jit(solution)/shard_map/all_to_all | solution.py:58
  106.6 10.7 %all-to-all-start.1 = ((bf16[16,64,1024]{2,1,0:T(8,128)(2,1)}), bf16[16,64,1024]{2,1,0:T(8,128)(2,1)S(1)}, u32[]{:S(2)}, u32[]{:S(2)}) async-start(bf16[16,64,1024]{2,1,0:T(8,128)(2,1)} %bitcast.24), calls=%async_computation.1 | async-start | bytes 4194304 | tf_op jit(solution)/shard_map/all_to_all | solution.py:57
  123.0 35.8 %all-to-all-done.1 = bf16[16,64,1024]{2,1,0:T(8,128)(2,1)S(1)} async-done(((bf16[16,64,1024]{2,1,0:T(8,128)(2,1)}), bf16[16,64,1024]{2,1,0:T(8,128)(2,1)S(1)}, u32[]{:S(2)}, u32[]{:S(2)}) %all-to-all-start.1) | async-done | bytes 2097184 | tf_op jit(solution)/shard_map/all_to_all | solution.py:57
  162.4 7.0 %maximum_select_fusion = (bf16[16,2,64,1024]{3,2,1,0:T(8,128)(2,1)S(1)}, bf16[16,2,64,1024]{3,2,1,0:T(8,128)(2,1)S(1)}) fusion(bf16[16,1,64,1024]{3,2,1,0:T(8,128)(2,1)} %bitcast.22, bf16[16,1,64,1024]{3,2,1,0:T(8,128)(2,1)} %bitcast.20, pred[]{:T(512)S(6)} %eq.16, bf16[16,1,64,1024]{3,2,1,0:T(8,128)(2,1)} %bitcast.27, bf16[16,1,64,1024]{3,2,1,0:T(8,128)(2,1)} %bitcast.29), kind=kLoop, calls=%fused_computation.66 | loop fusion | flops 12582912 | bytes 16777216 | tf_op jit(solution)/shard_map/jit(_where)/select_n | solution.py:66
  175.6 149.2 %while.10 = (s32[]{:T(128)}, bf16[2,8,64,8,128]{4,2,3,1,0:T(8,128)(2,1)}, s32[2,8,8]{1,0,2:T(2,128)S(1)}, bf16[32,64,8,128]{3,2,1,0:T(8,128)(2,1)}, pred[2,8,8]{...) while((s32[]{:T(128)}, ...), condition=%wide.region_3.5_spmd, body=%wide.region_0.4_spmd.sunk | while | flops 1099433984 | bytes 155246496 | solution.py:128
  175.8 7.6 %gather_fusion = bf16[64,64,8,128]{3,2,1,0:T(8,128)(2,1)} fusion(bf16[32,64,8,128]{3,2,1,0:T(8,128)(2,1)} %get-tuple-element.278, s32[1024]{0:T(1024)S(1)} %pad_clamp_fusion.2), kind=kCustom, calls=%fused_computation.1.clone.clone.1 | custom fusion | bytes 16777472 | tf_op jit(solution)/shard_map/while/body/eval_jaxpr/jit(_take)/gather | solution.py:112
  183.4 7.6 %gather_fusion.1 = bf16[64,64,8,128]{3,2,1,0:T(8,128)(2,1)} fusion(bf16[32,64,8,128]{3,2,1,0:T(8,128)(2,1)} %get-tuple-element.275, s32[1024]{0:T(1024)S(1)} %pad_clamp_fusion.2), kind=kCustom, calls=%fused_computation.clone.clone.1 | custom fusion | bytes 16777472 | tf_op jit(solution)/shard_map/while/body/eval_jaxpr/jit(_take)/gather | solution.py:115
  191.0 11.6 %broadcast_select_fusion.3 = (bf16[8,8,64,8,128]{4,3,2,1,0:T(8,128)(2,1)}, bf16[8,8,64,8,128]{4,3,2,1,0:T(8,128)(2,1)}) fusion(bf16[8,8,64,8,128]{4,3,2,1,0:T(8,128)(2,1)} %bitcast.131, pred[8,8]{1,0:T(8,128)(4,1)S(1)} %compare_and_fusion.2, bf16[8,8,64,8,128]{4,3,2,1,0:T(8,128)(2,1)} %bitcast.132), kind=kLoop, calls=%fused_computation.46.clone.1 | loop fusion | flops 8388608 | bytes 33554496 | tf_op jit(solution)/shard_map/while/body/eval_jaxpr/jit(_take)/select_n | solution.py:112
  202.7 9.0 %copy.96 = bf16[8,8,64,8,128]{4,2,1,3,0:T(8,128)(2,1)} copy(bf16[8,8,64,8,128]{4,3,2,1,0:T(8,128)(2,1)} %get-tuple-element.253) | data formatting | bytes 16777216 | tf_op jit(solution)/shard_map/while/body/eval_jaxpr/jit(_take)/select_n | solution.py:112
  211.7 9.6 %fusion.107 = f32[8,8,64,512]{3,2,1,0:T(8,128)} fusion(bf16[8,512,8,128]{3,1,2,0:T(8,128)(2,1)} %bitcast.133, bf16[1,8,64,8,128]{4,3,2,1,0:T(8,128)(2,1)S(1)} %constant_dynamic-slice_fusion.6), kind=kOutput, calls=%fused_computation.57.clone.1 | convolution fusion | flops 536870912 | bytes 17825792 | tf_op jit(solution)/shard_map/while/body/eval_jaxpr/pqhs,pkhs->phqk/dot_general | solution.py:118
  221.5 11.4 %fusion.108 = (f32[8,8,64]{2,1,0:T(8,128)S(1)}, f32[8,8,64,512]{3,2,1,0:T(8,128)}) fusion(f32[8,8,64,512]{3,2,1,0:T(8,128)} %fusion.107, pred[8,512]{1,0:T(8,128)(4,1)S(1)} %broadcast_in_dim.104), kind=kOutput, calls=%fused_computation.83.clone.1 | output fusion | flops 12583423 | bytes 16797696 | tf_op jit(solution)/shard_map/while/body/eval_jaxpr/sub | solution.py:26
  232.9 9.0 %copy.95 = bf16[8,8,64,8,128]{4,2,1,3,0:T(8,128)(2,1)} copy(bf16[8,8,64,8,128]{4,3,2,1,0:T(8,128)(2,1)} %get-tuple-element.252) | data formatting | bytes 16777216 | tf_op jit(solution)/shard_map/while/body/eval_jaxpr/jit(_take)/select_n | solution.py:115
  241.9 8.3 %fusion.109 = bf16[2,8,64,8,128]{4,2,3,1,0:T(8,128)(2,1)} fusion(bf16[2,8,64,8,128]{4,2,3,1,0:T(8,128)(2,1)} %get-tuple-element.265, s32[]{:T(128)} %get-tuple-element.264, bf16[8,512,8,128]{3,1,2,0:T(8,128)(2,1)} %bitcast.137, f32[8,8,64,512]{3,2,1,0:T(8,128)} %get-tuple-element.254, f32[8,8,64]{2,1,0:T(8,128)S(1)} %get-tuple-element.255), kind=kOutput, calls=%fused_computation.55.clone.1 | convolution fusion | flops 541589504 | bytes 17842688 | tf_op jit(solution)/shard_map/while/body/eval_jaxpr/phqk,pkhs->pqhs/dot_general | solution.py:124
  250.4 7.6 %gather_fusion = bf16[64,64,8,128]{3,2,1,0:T(8,128)(2,1)} fusion(bf16[32,64,8,128]{3,2,1,0:T(8,128)(2,1)} %get-tuple-element.278, s32[1024]{0:T(1024)S(1)} %pad_clamp_fusion.2), kind=kCustom, calls=%fused_computation.1.clone.clone.1 | custom fusion | bytes 16777472 | tf_op jit(solution)/shard_map/while/body/eval_jaxpr/jit(_take)/gather | solution.py:112
  258.0 7.6 %gather_fusion.1 = bf16[64,64,8,128]{3,2,1,0:T(8,128)(2,1)} fusion(bf16[32,64,8,128]{3,2,1,0:T(8,128)(2,1)} %get-tuple-element.275, s32[1024]{0:T(1024)S(1)} %pad_clamp_fusion.2), kind=kCustom, calls=%fused_computation.clone.clone.1 | custom fusion | bytes 16777472 | tf_op jit(solution)/shard_map/while/body/eval_jaxpr/jit(_take)/gather | solution.py:115
  265.6 11.6 %broadcast_select_fusion.3 = (bf16[8,8,64,8,128]{4,3,2,1,0:T(8,128)(2,1)}, bf16[8,8,64,8,128]{4,3,2,1,0:T(8,128)(2,1)}) fusion(bf16[8,8,64,8,128]{4,3,2,1,0:T(8,128)(2,1)} %bitcast.131, pred[8,8]{1,0:T(8,128)(4,1)S(1)} %compare_and_fusion.2, bf16[8,8,64,8,128]{4,3,2,1,0:T(8,128)(2,1)} %bitcast.132), kind=kLoop, calls=%fused_computation.46.clone.1 | loop fusion | flops 8388608 | bytes 33554496 | tf_op jit(solution)/shard_map/while/body/eval_jaxpr/jit(_take)/select_n | solution.py:112
  277.2 9.0 %copy.96 = bf16[8,8,64,8,128]{4,2,1,3,0:T(8,128)(2,1)} copy(bf16[8,8,64,8,128]{4,3,2,1,0:T(8,128)(2,1)} %get-tuple-element.253) | data formatting | bytes 16777216 | tf_op jit(solution)/shard_map/while/body/eval_jaxpr/jit(_take)/select_n | solution.py:112
  286.3 9.6 %fusion.107 = f32[8,8,64,512]{3,2,1,0:T(8,128)} fusion(bf16[8,512,8,128]{3,1,2,0:T(8,128)(2,1)} %bitcast.133, bf16[1,8,64,8,128]{4,3,2,1,0:T(8,128)(2,1)S(1)} %constant_dynamic-slice_fusion.6), kind=kOutput, calls=%fused_computation.57.clone.1 | convolution fusion | flops 536870912 | bytes 17825792 | tf_op jit(solution)/shard_map/while/body/eval_jaxpr/pqhs,pkhs->phqk/dot_general | solution.py:118
  296.1 11.4 %fusion.108 = (f32[8,8,64]{2,1,0:T(8,128)S(1)}, f32[8,8,64,512]{3,2,1,0:T(8,128)}) fusion(f32[8,8,64,512]{3,2,1,0:T(8,128)} %fusion.107, pred[8,512]{1,0:T(8,128)(4,1)S(1)} %broadcast_in_dim.104), kind=kOutput, calls=%fused_computation.83.clone.1 | output fusion | flops 12583423 | bytes 16797696 | tf_op jit(solution)/shard_map/while/body/eval_jaxpr/sub | solution.py:26
  307.5 9.0 %copy.95 = bf16[8,8,64,8,128]{4,2,1,3,0:T(8,128)(2,1)} copy(bf16[8,8,64,8,128]{4,3,2,1,0:T(8,128)(2,1)} %get-tuple-element.252) | data formatting | bytes 16777216 | tf_op jit(solution)/shard_map/while/body/eval_jaxpr/jit(_take)/select_n | solution.py:115
  316.4 8.3 %fusion.109 = bf16[2,8,64,8,128]{4,2,3,1,0:T(8,128)(2,1)} fusion(bf16[2,8,64,8,128]{4,2,3,1,0:T(8,128)(2,1)} %get-tuple-element.265, s32[]{:T(128)} %get-tuple-element.264, bf16[8,512,8,128]{3,1,2,0:T(8,128)(2,1)} %bitcast.137, f32[8,8,64,512]{3,2,1,0:T(8,128)} %get-tuple-element.254, f32[8,8,64]{2,1,0:T(8,128)S(1)} %get-tuple-element.255), kind=kOutput, calls=%fused_computation.55.clone.1 | convolution fusion | flops 541589504 | bytes 17842688 | tf_op jit(solution)/shard_map/while/body/eval_jaxpr/phqk,pkhs->pqhs/dot_general | solution.py:124
  324.8 17.7 %conditional.3 = (bf16[16,64,8,128]{3,1,2,0:T(8,128)(2,1)}) conditional(s32[]{:T(128)} %convert_element_type.33, bf16[16,64,8,128]{3,1,2,0:T(8,128)(2,1)} %get-tuple-element.280, (s32[]{:T(128)}, s32[]{:T(128)}, pred[]{:T(512)}, s32[]{:T(128)}, bf16[16,64,8,128]{3,2,1,0:T(8,128)(2,1)S(1)}, /*index=5*/bf16[2048,8,128]{2,1,0:T(8,128)(2,1)}, ...), branch_computations={%region_8.10_spmd, %region_9.13_spmd} | conditional | flops 812716544 | bytes 50729176 | solution.py:151
  328.3 3.5 fusion.39
  331.8 4.5 %fusion.89 = f32[8,64]{1,0:T(8,128)S(1)} fusion(bf16[2048,8,128]{2,1,0:T(8,128)(2,1)} %get-tuple-element.174, bf16[16,64,8,128]{3,1,2,0:T(8,128)(2,1)} %copy-done.6, s32[]{:T(128)S(6)} %select_n.70), kind=kOutput, calls=%fused_computation.82 | convolution fusion | flops 271583232 | bytes 4327428 | tf_op jit(solution)/shard_map/cond/branch_1_fun/sub | solution.py:26
  336.3 6.2 %fusion.50 = bf16[16,64,8,128]{3,1,2,0:T(8,128)(2,1)} fusion(bf16[16,64,8,128]{3,1,2,0:T(8,128)(2,1)} %get-tuple-element.100, s32[]{:T(128)S(6)} %select_n.70, bf16[2048,8,128]{2,1,0:T(8,128)(2,1)} %get-tuple-element.175, f32[8,64]{1,0:T(8,128)S(1)} %fusion.89, f32[8,64,2048]{2,1,0:T(8,128)} %fusion.39), kind=kOutput, calls=%fused_computation.35 | convolution fusion | flops 272697856 | bytes 8521732 | tf_op jit(solution)/shard_map/cond/branch_1_fun/hqk,khs->qhs/dot_general | solution.py:35
  344.4 76.0 %all_to_all.44 = bf16[16,64,1024]{2,1,0:T(8,128)(2,1)S(1)} all-to-all(bf16[16,64,1024]{2,1,0:T(8,128)(2,1)S(1)} %copy_bitcast_fusion.2), channel_id=1, replica_groups=mesh['groups'=2,'seq'=16] {'seq'}, dimensions={0} | all-to-all | bytes 4194304 | tf_op jit(solution)/shard_map/all_to_all | solution.py:152
  (68 shorter events, 27.8 us)
Async XLA Ops:
  0.0 122.1 %copy-start = (s32[2,32,3]{1,0,2:T(2,128)S(1)}, s32[2,32,3]{1,0,2:T(2,128)}, u32[]{:S(2)}) copy-start(s32[2,32,3]{1,0,2:T(2,128)} %param.16) | copy-start | bytes 2308
  5.3 49.0 %all-to-all-start = ((bf16[16,64,1024]{2,1,0:T(8,128)(2,1)}), bf16[16,64,1024]{2,1,0:T(8,128)(2,1)}, u32[]{:S(2)}, u32[]{:S(2)}) async-start(bf16[16,64,1024]{2,1,0:T(8,128)(2,1)} %bitcast.19), calls=%async_computation | async-start | bytes 4194304 | tf_op jit(solution)/shard_map/all_to_all | solution.py:59
  54.3 52.3 %all-to-all-start.2 = ((bf16[16,64,1024]{2,1,0:T(8,128)(2,1)}), bf16[16,64,1024]{2,1,0:T(8,128)(2,1)}, u32[]{:S(2)}, u32[]{:S(2)}) async-start(bf16[16,64,1024]{2,1,0:T(8,128)(2,1)} %bitcast.26), calls=%async_computation.2 | async-start | bytes 4194304 | tf_op jit(solution)/shard_map/all_to_all | solution.py:58
  68.3 49.5 %copy-start.7 = (s32[2,2]{1,0:T(2,128)S(1)}, s32[2,2]{1,0:T(2,128)}, u32[]{:S(2)}) copy-start(s32[2,2]{1,0:T(2,128)} %param.17) | copy-start | bytes 52
  106.6 52.2 %all-to-all-start.1 = ((bf16[16,64,1024]{2,1,0:T(8,128)(2,1)}), bf16[16,64,1024]{2,1,0:T(8,128)(2,1)S(1)}, u32[]{:S(2)}, u32[]{:S(2)}) async-start(bf16[16,64,1024]{2,1,0:T(8,128)(2,1)} %bitcast.24), calls=%async_computation.1 | async-start | bytes 4194304 | tf_op jit(solution)/shard_map/all_to_all | solution.py:57
  117.2 45.1 %collective-permute-start = (bf16[1,1024,1024]{2,1,0:T(8,128)(2,1)}, bf16[1,1024,1024]{2,1,0:T(8,128)(2,1)}, u32[]{:S(2)}, u32[]{:S(2)}) collective-permute-start(bf16[1,1024,1024]{2,1,0:T(8,128)(2,1)} %bitcast.21), channel_id=1, source_target_pairs={{0,1},{1,0},{2,3},{3,2},{4,5},{5,4},{6,7},{7,6},{8,9},{9,8},{10,11... | collective-permute-start | bytes 6291464 | tf_op jit(solution)/shard_map/ppermute | solution.py:21
  117.4 45.0 %collective-permute-start.1 = (bf16[1,1024,1024]{2,1,0:T(8,128)(2,1)}, bf16[1,1024,1024]{2,1,0:T(8,128)(2,1)}, u32[]{:S(2)}, u32[]{:S(2)}) collective-permute-start(bf16[1,1024,1024]{2,1,0:T(8,128)(2,1)} %bitcast.28), channel_id=1, source_target_pairs={{0,1},{1,0},{2,3},{3,2},{4,5},{5,4},{6,7},{7,6},{8,9},{9,8},{10,11... | collective-permute-start | bytes 6291464 | tf_op jit(solution)/shard_map/ppermute | solution.py:21
  158.8 1.4 copy-start.4
  325.3 2.9 copy-start.3
  326.0 1.3 copy-start.6
  420.5 4.4 %copy-start.1 = (s32[2,32,3]{1,0,2:T(2,128)S(1)}, s32[2,32,3]{1,0,2:T(2,128)}, u32[]{:S(2)}) copy-start(s32[2,32,3]{1,0,2:T(2,128)} %param.16) | copy-start | bytes 2308
where the time goes:
time: 417 us; the launch traced here: 425 us
  waiting for transfers between devices  108 us (26%)
  local copies, waits for them, and re-layouts  104 us (25%)
  blocking collectives  76 us (18%)
  other arithmetic  53.2 us (13%)
  matrix products  50.1 us (12%)
  starting transfers between devices  29.2 us (7%)
    all_to_all x1, blocking collectives, per_device(): lax.all_to_all(attended.reshape(devices, block_len, group_width), 'seq',...  76 us
    all_to_all x1, waiting for transfers between devices, per_device(): lax.all_to_all(by_parity(value_states), 'seq', split_axis=0, concat_axis=...  36.3 us
    all_to_all x1, waiting for transfers between devices, per_device(): lax.all_to_all(by_parity(key_states), 'seq', split_axis=0, concat_axis=1,...  36.3 us
    all_to_all x1, waiting for transfers between devices, per_device(): lax.all_to_all(by_parity(queries), 'seq', split_axis=0, concat_axis=1, ti...  35.8 us
    select_n x2, other arithmetic, local_group(): jnp.take(key_blocks, listed_group, axis=0)  23.2 us
    sub x2, other arithmetic, soft_weights(): exponent = jnp.exp(scores - row_max)  22.8 us
    dot_general x2, matrix products, local_group(): jnp.einsum('pqhs,pkhs->phqk', query_group, gathered_keys, preferred_eleme...  19.2 us
    select_n x2, local copies, waits for them, and re-layouts, local_group(): jnp.take(value_blocks, listed_group, axis=0)  17.9 us
  transfers between devices with their start and end apart: 5, of which 3 were waited for; matrix products, arithmetic and copies ran while one was open for 3% of the time, Pallas kernels for 0%

commit v1 on v0

v1 whole, which is shorter than its diff:
```python
import functools
import math

import jax
import jax.numpy as jnp
from jax import lax
from jax.experimental import pallas as pl
from jax.experimental.pallas import tpu as pltpu
from jax.sharding import PartitionSpec as P

HEAD_DIM = 128
BLOCK = 64
NGLOB = 2
NRAND = 3


def from_partner(block, axis, distance):
    count = lax.axis_size(axis)
    route = []
    for low in range(count):
        high = low | 1 << distance
        if high != low and high < count:
            route += [(low, high), (high, low)]
    return lax.ppermute(block, axis, route)


def attend_kernel(total_blocks, listed, info, q_ref, ko_ref, kt_ref, vo_ref, vt_ref, o_ref, k_all, v_all):
    rows = q_ref.shape[0]
    count = rows // BLOCK
    width = NGLOB + 3 + NRAND
    scale = HEAD_DIM ** (-0.5)
    k_all[pl.ds(0, rows), :] = ko_ref[...]
    k_all[pl.ds(rows, rows), :] = kt_ref[...]
    v_all[pl.ds(0, rows), :] = vo_ref[...]
    v_all[pl.ds(rows, rows), :] = vt_ref[...]
    parity = info[0]
    per_step = math.gcd(count, 4)
    column = lax.broadcasted_iota(jnp.int32, (BLOCK, width * BLOCK), 1) // BLOCK
    contract = (((1,), (1,)), ((), ()))

    def gather(ref, place):
        parts = []
        for slot in range(width):
            at = pl.multiple_of(listed[place * width + slot] * BLOCK, BLOCK)
            parts.append(ref[pl.ds(at, BLOCK), :])
        return jnp.concatenate(parts, axis=0)

    def step(index, carry):
        places = [index * per_step + sub for sub in range(per_step)]
        scores = []
        for place in places:
            query = q_ref[pl.ds(pl.multiple_of(place * BLOCK, BLOCK), BLOCK), :]
            score = lax.dot_general(query, gather(k_all, place), contract, preferred_element_type=jnp.float32)
            position = 2 * place + parity
            dead = jnp.where(position == 0, NGLOB, jnp.where(position == total_blocks - 1, NGLOB + 2, -1))
            scores.append(jnp.where(column == dead, -1e30, score))
        results = []
        for place, score in zip(places, scores):
            exponent = jnp.exp((score - jnp.max(score, axis=1, keepdims=True)) * scale)
            total = jnp.sum(exponent, axis=1, keepdims=True)
            weights = exponent.astype(jnp.bfloat16)
            summed = jnp.dot(weights, gather(v_all, place), preferred_element_type=jnp.float32)
            results.append((summed / total).astype(jnp.bfloat16))
        for place, result in zip(places, results):
            o_ref[pl.ds(pl.multiple_of(place * BLOCK, BLOCK), BLOCK), :] = result
        return carry

    lax.fori_loop(0, count // per_step, step, 0)
    chunk = math.gcd(2 * rows, 1024)
    for slot in range(NGLOB):
        block = info[1 + slot]

        @pl.when(block % 2 == parity)
        def _():
            at = pl.multiple_of((block // 2) * BLOCK, BLOCK)
            query = q_ref[pl.ds(at, BLOCK), :]

            def part(index, carry):
                top, total, summed = carry
                here = pl.ds(pl.multiple_of(index * chunk, chunk), chunk)
                score = lax.dot_general(query, k_all[here, :], contract, preferred_element_type=jnp.float32)
                new_top = jnp.maximum(top, jnp.max(score, axis=1, keepdims=True))
                shrink = jnp.exp((top - new_top) * scale)
                exponent = jnp.exp((score - new_top) * scale)
                total = total * shrink + jnp.sum(exponent, axis=1, keepdims=True)
                summed = summed * shrink + jnp.dot(
                    exponent.astype(jnp.bfloat16), v_all[here, :], preferred_element_type=jnp.float32
                )
                return new_top, total, summed

            start = (
                jnp.full((BLOCK, 1), -1e30, jnp.float32),
                jnp.zeros((BLOCK, 1), jnp.float32),
                jnp.zeros((BLOCK, HEAD_DIM), jnp.float32),
            )
            _, total, summed = lax.fori_loop(0, 2 * rows // chunk, part, start)
            o_ref[pl.ds(at, BLOCK), :] = (summed / total).astype(jnp.bfloat16)


def per_device(queries, key_states, value_states, random_blocks, global_blocks):
    devices = lax.axis_size("seq")
    device = lax.axis_index("seq")
    documents = queries.shape[0]
    head_groups = devices // (2 * documents)
    group_width = queries.shape[2] // head_groups
    heads_here = group_width // HEAD_DIM
    block_len = BLOCK
    total_blocks = 2 * devices
    parity = device % 2
    document = device // (2 * head_groups)

    def by_parity(states):
        pieces = states.reshape(documents, 2, block_len, head_groups, group_width)
        return pieces.transpose(0, 3, 1, 2, 4).reshape(devices, block_len, group_width)

    query_recv, key_half, value_half = (
        lax.all_to_all(by_parity(queries), "seq", split_axis=0, concat_axis=1, tiled=True),
        lax.all_to_all(by_parity(key_states), "seq", split_axis=0, concat_axis=1, tiled=True),
        lax.all_to_all(by_parity(value_states), "seq", split_axis=0, concat_axis=1, tiled=True),
    )
    key_other, value_other = from_partner((key_half, value_half), "seq", 0)

    document_lists = lax.dynamic_index_in_dim(random_blocks, document, 0, keepdims=False)
    own_lists = lax.dynamic_index_in_dim(
        document_lists.reshape(devices, 2, NRAND), parity, 1, keepdims=False
    )
    globals_here = lax.dynamic_index_in_dim(global_blocks, document, 0, keepdims=False)
    positions = 2 * jnp.arange(devices, dtype=jnp.int32) + parity
    listed = jnp.concatenate(
        [
            jnp.broadcast_to(globals_here[None, :], (devices, NGLOB)),
            (positions - 1)[:, None],
            positions[:, None],
            (positions + 1)[:, None],
            own_lists,
        ],
        axis=1,
    )
    listed = jnp.clip(listed, 0, total_blocks - 1)
    listed = listed // 2 + jnp.where(listed % 2 == parity, 0, devices)
    info = jnp.concatenate([jnp.reshape(parity, (1,)), globals_here]).astype(jnp.int32)
    rows = devices * block_len
    column_block = pl.BlockSpec((rows, HEAD_DIM), lambda head, *_: (0, head))
    attended = pl.pallas_call(
        functools.partial(attend_kernel, total_blocks),
        out_shape=jax.ShapeDtypeStruct((rows, group_width), jnp.bfloat16),
        grid_spec=pltpu.PrefetchScalarGridSpec(
            num_scalar_prefetch=2,
            grid=(heads_here,),
            in_specs=[column_block] * 5,
            out_specs=column_block,
            scratch_shapes=[pltpu.VMEM((2 * rows, HEAD_DIM), jnp.bfloat16)] * 2,
        ),
    )(
        listed.reshape(-1).astype(jnp.int32),
        info,
        query_recv.reshape(rows, group_width),
        key_half.reshape(rows, group_width),
        key_other.reshape(rows, group_width),
        value_half.reshape(rows, group_width),
        value_other.reshape(rows, group_width),
    )
    returned = lax.all_to_all(
        attended.reshape(devices, block_len, group_width),
        "seq",
        split_axis=0,
        concat_axis=0,
        tiled=True,
    )
    returned = returned.reshape(documents, head_groups, 2, block_len, group_width).transpose(
        0, 2, 3, 1, 4
    )
    return returned.reshape(documents, 2 * block_len, head_groups * group_width)


def solution(mesh):
    placed = (
        P("groups", "seq", None),
        P("groups", "seq", None),
        P("groups", "seq", None),
        P("groups", None, None),
        P("groups", None),
    )
    return jax.shard_map(
        per_device, mesh=mesh, in_specs=placed, out_specs=P("groups", "seq", None), check_vma=False
    )
```

time: 417 us -> 261 us (0.63); the launches traced: 425 us -> 261 us
  local copies, waits for them, and re-layouts: 104 us -> 29.4 us
  other arithmetic: 53.2 us -> 1.23 us
  matrix products: 50.1 us -> 0 us
  Pallas kernels: 0 us -> 36.8 us
  blocking collectives: 76 us -> 57.5 us
    dot_general x6 -> x0, matrix products: 45.6 us -> none  [the longest x2 19.2 us: local_group(): jnp.einsum('pqhs,pkhs->phqk', query_group, gathered_keys, preferred_eleme...]
    pallas_call x0 -> x1, Pallas kernels: none -> 36.8 us  [per_device(): pl.pallas_call(functools.partial(attend_kernel, total_blocks), out_shape=...]
    select_n x4 -> x0, local copies, waits for them, and re-layouts: 35.9 us -> none  [the longest x2 17.9 us: local_group(): jnp.take(value_blocks, listed_group, axis=0)]
    gather x4 -> x0, local copies, waits for them, and re-layouts: 30.5 us -> none  [the longest x2 15.3 us: local_group(): jnp.take(key_blocks, listed_group, axis=0)]
    select_n x5 -> x0, other arithmetic: 30.3 us -> none  [the longest x2 23.2 us: local_group(): jnp.take(key_blocks, listed_group, axis=0)]
    sub x2 -> x1, other arithmetic: 22.8 us -> 0.01 us  [per_device(): positions - 1]
    all_to_all x1, blocking collectives: 76 us -> 57.5 us  [per_device(): lax.all_to_all(attended.reshape(devices, block_len, group_width), 'seq',...]
    unnamed x12 -> x6, local copies, waits for them, and re-layouts: 9.85 us -> 0.01 us
  transfers between devices with their start and end apart: 5 -> 5, of which waited for: 3 -> 3; matrix products, arithmetic and copies ran while one was open for 3% -> 7% of each run, Pallas kernels for 0% -> 0%
where the time goes in v1:
time: 261 us
  waiting for transfers between devices  106 us (41%)
  blocking collectives  57.5 us (22%)
  Pallas kernels  36.8 us (14%)
  local copies, waits for them, and re-layouts  29.4 us (11%)
  starting transfers between devices  29.3 us (11%)
    all_to_all x1, blocking collectives, per_device(): lax.all_to_all(attended.reshape(devices, block_len, group_width), 'seq',...  57.5 us
    all_to_all x1, waiting for transfers between devices, per_device(): lax.all_to_all(by_parity(queries), 'seq', split_axis=0, concat_axis=1, ti...  39.3 us
    pallas_call x1, Pallas kernels, per_device(): pl.pallas_call(functools.partial(attend_kernel, total_blocks), out_shape=...  36.8 us
    all_to_all x1, waiting for transfers between devices, per_device(): lax.all_to_all(by_parity(value_states), 'seq', split_axis=0, concat_axis=...  33.6 us
    all_to_all x1, waiting for transfers between devices, per_device(): lax.all_to_all(by_parity(key_states), 'seq', split_axis=0, concat_axis=1,...  33.5 us
    reshape x3, local copies, waits for them, and re-layouts, by_parity(): pieces = states.reshape(documents, 2, block_len, head_groups, group_width)  12.3 us
    all_to_all x1, starting transfers between devices, per_device(): lax.all_to_all(by_parity(queries), 'seq', split_axis=0, concat_axis=1, ti...  10.8 us
    all_to_all x1, starting transfers between devices, per_device(): lax.all_to_all(by_parity(value_states), 'seq', split_axis=0, concat_axis=...  10.7 us
  transfers between devices with their start and end apart: 5, of which 3 were waited for; matrix products, arithmetic and copies ran while one was open for 7% of the time, Pallas kernels for 0%

profile of v1, /device:TPU:1, one launch (start us, length us, event | category | flops | bytes accessed | tf_op | source)
XLA Modules:
  0.0 260.7 jit_solution(11194658292195489300)
XLA Ops:
  0.0 0.0 copy-start
  0.0 3.3 %reshape.91 = bf16[2,2,64,4,1024]{4,3,2,1,0:T(4,128)(2,1)S(1)} reshape(bf16[2,128,4096]{2,1,0:T(8,128)(2,1)} %param.6) | data formatting | bytes 4194304 | tf_op jit(solution)/shard_map/reshape | solution.py:113
  3.3 2.0 copy.13
  5.3 7.3 %all-to-all-start.1 = ((bf16[16,64,1024]{2,1,0:T(8,128)(2,1)}), bf16[16,64,1024]{2,1,0:T(8,128)(2,1)S(1)}, u32[]{:S(2)}, u32[]{:S(2)}) async-start(bf16[16,64,1024]{2,1,0:T(8,128)(2,1)} %bitcast.28), calls=%async_computation.1 | async-start | bytes 4194304 | tf_op jit(solution)/shard_map/all_to_all | solution.py:118
  12.6 4.5 %reshape.95 = bf16[2,2,64,4,1024]{4,3,2,1,0:T(4,128)(2,1)} reshape(bf16[2,128,4096]{2,1,0:T(8,128)(2,1)} %param.7) | data formatting | bytes 4194304 | tf_op jit(solution)/shard_map/reshape | solution.py:113
  17.1 3.5 %copy.14 = bf16[2,4,2,64,1024]{4,3,2,1,0:T(8,128)(2,1)} copy(bf16[2,4,2,64,1024]{4,1,3,2,0:T(4,128)(2,1)} %bitcast.32) | data formatting | bytes 4194304 | tf_op jit(solution)/shard_map/transpose | solution.py:114
  20.7 33.5 %all-to-all-done.1 = bf16[16,64,1024]{2,1,0:T(8,128)(2,1)S(1)} async-done(((bf16[16,64,1024]{2,1,0:T(8,128)(2,1)}), bf16[16,64,1024]{2,1,0:T(8,128)(2,1)S(1)}, u32[]{:S(2)}, u32[]{:S(2)}) %all-to-all-start.1) | async-done | bytes 2097184 | tf_op jit(solution)/shard_map/all_to_all | solution.py:118
  54.2 0.0 copy-start.1
  54.2 10.7 %all-to-all-start.2 = ((bf16[16,64,1024]{2,1,0:T(8,128)(2,1)}), bf16[16,64,1024]{2,1,0:T(8,128)(2,1)}, u32[]{:S(2)}, u32[]{:S(2)}) async-start(bf16[16,64,1024]{2,1,0:T(8,128)(2,1)} %bitcast.27), calls=%async_computation.2 | async-start | bytes 4194304 | tf_op jit(solution)/shard_map/all_to_all | solution.py:119
  64.8 4.5 %reshape.88 = bf16[2,2,64,4,1024]{4,3,2,1,0:T(4,128)(2,1)} reshape(bf16[2,128,4096]{2,1,0:T(8,128)(2,1)} %param.5) | data formatting | bytes 4194304 | tf_op jit(solution)/shard_map/reshape | solution.py:113
  69.3 3.6 %copy.12 = bf16[2,4,2,64,1024]{4,3,2,1,0:T(8,128)(2,1)} copy(bf16[2,4,2,64,1024]{4,1,3,2,0:T(4,128)(2,1)} %bitcast.33) | data formatting | bytes 4194304 | tf_op jit(solution)/shard_map/transpose | solution.py:114
  72.9 33.6 %all-to-all-done.2 = bf16[16,64,1024]{2,1,0:T(8,128)(2,1)} async-done(((bf16[16,64,1024]{2,1,0:T(8,128)(2,1)}), bf16[16,64,1024]{2,1,0:T(8,128)(2,1)}, u32[]{:S(2)}, u32[]{:S(2)}) %all-to-all-start.2) | async-done | bytes 2097184 | tf_op jit(solution)/shard_map/all_to_all | solution.py:119
  106.5 10.8 %all-to-all-start = ((bf16[16,64,1024]{2,1,0:T(8,128)(2,1)}), bf16[16,64,1024]{2,1,0:T(8,128)(2,1)}, u32[]{:S(2)}, u32[]{:S(2)}) async-start(bf16[16,64,1024]{2,1,0:T(8,128)(2,1)} %bitcast.26), calls=%async_computation | async-start | bytes 4194304 | tf_op jit(solution)/shard_map/all_to_all | solution.py:117
  117.3 0.2 collective-permute-start.1
  117.5 0.0 copy-done.1
  117.5 0.3 collective-permute-start
  117.8 0.0 copy-done
  117.8 0.1 reshape.86
  117.9 0.2 dynamic-slice_reduce_fusion
  118.1 0.0 copy-done.2
  118.2 0.1 broadcast_in_dim.18
  118.3 0.1 copy.11
  118.4 0.1 min.12
  118.4 0.6 pad_add_fusion.info
  119.1 0.6 fusion.1.listed
  119.7 39.3 %all-to-all-done = bf16[16,64,1024]{2,1,0:T(8,128)(2,1)} async-done(((bf16[16,64,1024]{2,1,0:T(8,128)(2,1)}), bf16[16,64,1024]{2,1,0:T(8,128)(2,1)}, u32[]{:S(2)}, u32[]{:S(2)}) %all-to-all-start) | async-done | bytes 2097184 | tf_op jit(solution)/shard_map/all_to_all | solution.py:117
  158.9 0.0 collective-permute-done.1
  158.9 0.0 collective-permute-done
  158.9 36.8 %shard_map.55 = bf16[1024,1024]{1,0:T(8,128)(2,1)} custom-call(s32[128]{0:T(128)} %fusion.1.listed, s32[3]{0:T(128)} %pad_add_fusion.info, bf16[1024,1024]{1,0:T(8,128)(2,1)} %bitcast.4.q_ref, bf16[1024,1024]{1,0:T(8,128)(2,1)} %bitcast.24, bf16[1024,1024]{1,0:T(8,128)(2,1)} %bitcast.9.kt_ref, bf16[1024,1024]{1,0:T(8,128)(2,1)} %bitcast.12.vo_ref, ...), custom_call_target="tpu_custom_call" | custom-call | tf_op jit(solution)/shard_map/pallas_call | solution.py:144
  195.7 57.5 %all_to_all.38 = bf16[16,64,1024]{2,1,0:T(8,128)(2,1)S(1)} all-to-all(bf16[16,64,1024]{2,1,0:T(8,128)(2,1)} %bitcast.25), channel_id=1, replica_groups=mesh['groups'=2,'seq'=16] {'seq'}, dimensions={0} | all-to-all | bytes 4194304 | tf_op jit(solution)/shard_map/all_to_all | solution.py:163
  253.3 3.0 %copy.17 = bf16[2,4,2,64,1024]{4,1,3,2,0:T(4,128)(2,1)} copy(bf16[2,4,2,64,1024]{4,3,2,1,0:T(8,128)(2,1)S(1)} %bitcast.29) | data formatting | bytes 4194304 | tf_op jit(solution)/shard_map/reshape | solution.py:170
  256.2 4.5 %reshape.101 = bf16[2,128,4096]{2,1,0:T(8,128)(2,1)} reshape(bf16[2,2,64,4,1024]{4,3,2,1,0:T(4,128)(2,1)} %bitcast.30) | data formatting | bytes 4194304 | tf_op jit(solution)/shard_map/reshape | solution.py:173
  (7 shorter events, 0.1 us)
Async XLA Ops:
  0.0 117.8 %copy-start = (s32[2,32,3]{1,0,2:T(2,128)S(1)}, s32[2,32,3]{1,0,2:T(2,128)}, u32[]{:S(2)}) copy-start(s32[2,32,3]{1,0,2:T(2,128)} %param.8) | copy-start | bytes 2308
  5.3 48.9 %all-to-all-start.1 = ((bf16[16,64,1024]{2,1,0:T(8,128)(2,1)}), bf16[16,64,1024]{2,1,0:T(8,128)(2,1)S(1)}, u32[]{:S(2)}, u32[]{:S(2)}) async-start(bf16[16,64,1024]{2,1,0:T(8,128)(2,1)} %bitcast.28), calls=%async_computation.1 | async-start | bytes 4194304 | tf_op jit(solution)/shard_map/all_to_all | solution.py:118
  54.2 63.3 %copy-start.1 = (bf16[16,64,1024]{2,1,0:T(8,128)(2,1)}, bf16[16,64,1024]{2,1,0:T(8,128)(2,1)S(1)}, u32[]{:S(2)}) copy-start(bf16[16,64,1024]{2,1,0:T(8,128)(2,1)S(1)} %all-to-all-done.1) | copy-start | bytes 6291460
  54.2 52.3 %all-to-all-start.2 = ((bf16[16,64,1024]{2,1,0:T(8,128)(2,1)}), bf16[16,64,1024]{2,1,0:T(8,128)(2,1)}, u32[]{:S(2)}, u32[]{:S(2)}) async-start(bf16[16,64,1024]{2,1,0:T(8,128)(2,1)} %bitcast.27), calls=%async_computation.2 | async-start | bytes 4194304 | tf_op jit(solution)/shard_map/all_to_all | solution.py:119
  106.5 11.7 %copy-start.2 = (s32[2,2]{1,0:T(2,128)S(1)}, s32[2,2]{1,0:T(2,128)}, u32[]{:S(2)}) copy-start(s32[2,2]{1,0:T(2,128)} %param.9) | copy-start | bytes 52
  106.5 52.4 %all-to-all-start = ((bf16[16,64,1024]{2,1,0:T(8,128)(2,1)}), bf16[16,64,1024]{2,1,0:T(8,128)(2,1)}, u32[]{:S(2)}, u32[]{:S(2)}) async-start(bf16[16,64,1024]{2,1,0:T(8,128)(2,1)} %bitcast.26), calls=%async_computation | async-start | bytes 4194304 | tf_op jit(solution)/shard_map/all_to_all | solution.py:117
  117.3 41.6 %collective-permute-start.1 = (bf16[1,1024,1024]{2,1,0:T(8,128)(2,1)}, bf16[1,1024,1024]{2,1,0:T(8,128)(2,1)}, u32[]{:S(2)}, u32[]{:S(2)}) collective-permute-start(bf16[1,1024,1024]{2,1,0:T(8,128)(2,1)} %bitcast.13), channel_id=1, source_target_pairs={{0,1},{1,0},{2,3},{3,2},{4,5},{5,4},{6,7},{7,6},{8,9},{9,8},{10,11... | collective-permute-start | bytes 6291464 | tf_op jit(solution)/shard_map/ppermute | solution.py:24
  117.5 41.4 %collective-permute-start = (bf16[1,1024,1024]{2,1,0:T(8,128)(2,1)S(1)}, bf16[1,1024,1024]{2,1,0:T(8,128)(2,1)}, u32[]{:S(2)}, u32[]{:S(2)}) collective-permute-start(bf16[1,1024,1024]{2,1,0:T(8,128)(2,1)S(1)} %bitcast.23), channel_id=1, source_target_pairs={{0,1},{1,0},{2,3},{3,2},{4,5},{5,4},{6,7},{7,6},{8,9},{9,8},{10,11... | collective-permute-start | bytes 6291464 | tf_op jit(solution)/shard_map/ppermute | solution.py:24

commit v2 on v1

--- a/solution.py
+++ b/solution.py
@@ -95,6 +95,207 @@
             )
             _, total, summed = lax.fori_loop(0, 2 * rows // chunk, part, start)
             o_ref[pl.ds(at, BLOCK), :] = (summed / total).astype(jnp.bfloat16)
+
+
+def fused_kernel(
+    documents, chunk_count, listed, info, chosen, q_hbm, k_hbm, v_hbm, out_hbm, *scratch
+):
+    landed, made = scratch[:chunk_count], scratch[chunk_count : 2 * chunk_count]
+    send_sem, recv_sem, back_send_sem, back_recv_sem = scratch[2 * chunk_count :]
+    devices = lax.axis_size("seq")
+    me = lax.axis_index("seq")
+    head_groups = devices // documents
+    held_blocks = q_hbm.shape[1]
+    count = devices * held_blocks
+    chunk_width = landed[0].shape[3]
+    group_width = chunk_width * chunk_count
+    width = NGLOB + 3 + NRAND
+    scale = HEAD_DIM ** (-0.5)
+    sources = (k_hbm, v_hbm, q_hbm)
+
+    def outward(target, chunk):
+        column = pl.multiple_of(lax.rem(target, head_groups) * group_width + chunk * chunk_width, HEAD_DIM)
+        return lax.div(target, head_groups), pl.ds(column, chunk_width)
+
+    def blocks_of(device):
+        return pl.ds(device * held_blocks, held_blocks)
+
+    barrier = pltpu.get_barrier_semaphore()
+
+    def greet(step, carry):
+        pl.semaphore_signal(
+            barrier, inc=1, device_id={"seq": lax.rem(me + step, devices)}, device_id_type=pl.DeviceIdType.MESH
+        )
+        return carry
+
+    lax.fori_loop(1, devices, greet, 0)
+    pl.semaphore_wait(barrier, devices - 1)
+
+    for chunk in range(chunk_count):
+
+        def send(step, carry):
+            target = lax.rem(me + step, devices)
+            document, columns = outward(target, chunk)
+            for which, source in enumerate(sources):
+                pltpu.make_async_remote_copy(
+                    src_ref=source.at[document, :, :, columns],
+                    dst_ref=landed[chunk].at[which, blocks_of(me)],
+                    send_sem=send_sem.at[chunk],
+                    recv_sem=recv_sem.at[chunk],
+                    device_id={"seq": target},
+                    device_id_type=pl.DeviceIdType.MESH,
+                ).start()
+            return carry
+
+        lax.fori_loop(1, devices, send, 0)
+        document, columns = outward(me, chunk)
+        for which, source in enumerate(sources):
+            pltpu.make_async_copy(
+                source.at[document, :, :, columns], landed[chunk].at[which, blocks_of(me)], recv_sem.at[chunk]
+            ).start()
+
+    per_step = math.gcd(count, 4)
+    column_block = lax.broadcasted_iota(jnp.int32, (BLOCK, width * BLOCK), 1) // BLOCK
+    contract = (((1,), (1,)), ((), ()))
+    long_chunk = math.gcd(count, 16)
+
+    def attend(held, result_ref, head):
+        lanes = slice(head * HEAD_DIM, (head + 1) * HEAD_DIM)
+
+        def gather(which, place):
+            parts = []
+            for slot in range(width):
+                parts.append(held[which, listed[place * width + slot], :, lanes])
+            return jnp.concatenate(parts, axis=0)
+
+        global_results = []
+        for slot in range(NGLOB):
+            query = held[2, info[slot], :, lanes]
+            top = jnp.full((BLOCK, 1), -1e30, jnp.float32)
+            total = jnp.zeros((BLOCK, 1), jnp.float32)
+            summed = jnp.zeros((BLOCK, HEAD_DIM), jnp.float32)
+            for start in range(0, count, long_chunk):
+                here = slice(start, start + long_chunk)
+                score = lax.dot_general(query, held[0, here, :, lanes].reshape(-1, HEAD_DIM), contract, preferred_element_type=jnp.float32)
+                new_top = jnp.maximum(top, jnp.max(score, axis=1, keepdims=True))
+                shrink = jnp.exp((top - new_top) * scale)
+                exponent = jnp.exp((score - new_top) * scale)
+                total = total * shrink + jnp.sum(exponent, axis=1, keepdims=True)
+                summed = summed * shrink + jnp.dot(
+                    exponent.astype(jnp.bfloat16), held[1, here, :, lanes].reshape(-1, HEAD_DIM), preferred_element_type=jnp.float32
+                )
+                top = new_top
+            global_results.append(summed / total)
+
+        def step(index, carry):
+            places = [index * per_step + sub for sub in range(per_step)]
+            scores = []
+            for place in places:
+                query = held[2, place, :, lanes]
+                score = lax.dot_general(query, gather(0, place), contract, preferred_element_type=jnp.float32)
+                dead = jnp.where(place == 0, NGLOB, jnp.where(place == count - 1, NGLOB + 2, -1))
+                scores.append(jnp.where(column_block == dead, -1e30, score))
+            results = []
+            for place, score in zip(places, scores):
+                exponent = jnp.exp((score - jnp.max(score, axis=1, keepdims=True)) * scale)
+                total = jnp.sum(exponent, axis=1, keepdims=True)
+                summed = jnp.dot(exponent.astype(jnp.bfloat16), gather(1, place), preferred_element_type=jnp.float32)
+                result = summed / total
+                result = result * chosen[place * (NGLOB + 1) + NGLOB]
+                for slot in range(NGLOB):
+                    result += global_results[slot] * chosen[place * (NGLOB + 1) + slot]
+                results.append(result.astype(jnp.bfloat16))
+            for place, result in zip(places, results):
+                result_ref[place, :, lanes] = result
+            return carry
+
+        lax.fori_loop(0, count // per_step, step, 0)
+
+    def give_back(chunk):
+        document, columns = outward(me, chunk)
+
+        def send(step, carry):
+            target = lax.rem(me + step, devices)
+            pltpu.make_async_remote_copy(
+                src_ref=made[chunk].at[blocks_of(target)],
+                dst_ref=out_hbm.at[document, :, :, columns],
+                send_sem=back_send_sem.at[chunk],
+                recv_sem=back_recv_sem,
+                device_id={"seq": target},
+                device_id_type=pl.DeviceIdType.MESH,
+            ).start()
+            return carry
+
+        lax.fori_loop(1, devices, send, 0)
+        pltpu.make_async_copy(made[chunk].at[blocks_of(me)], out_hbm.at[document, :, :, columns], back_recv_sem).start()
+
+    for chunk in range(chunk_count):
+        pltpu.make_async_copy(landed[chunk], landed[chunk], recv_sem.at[chunk]).wait()
+        for head in range(chunk_width // HEAD_DIM):
+            attend(landed[chunk], made[chunk], head)
+        give_back(chunk)
+    others = pl.ds(0, count - held_blocks)
+    for chunk in range(chunk_count):
+        sent = landed[chunk].at[:, others]
+        pltpu.make_async_copy(sent, sent, send_sem.at[chunk]).wait()
+        sent = made[chunk].at[others]
+        pltpu.make_async_copy(sent, sent, back_send_sem.at[chunk]).wait()
+    pltpu.make_async_copy(out_hbm, out_hbm, back_recv_sem).wait()
+
+
+CHUNK_HEADS = 1
+
+
+def per_device_fused(queries, key_states, value_states, random_blocks, global_blocks):
+    devices = lax.axis_size("seq")
+    documents, tokens, features = queries.shape
+    head_groups = devices // documents
+    group_width = features // head_groups
+    chunk_width = CHUNK_HEADS * HEAD_DIM
+    chunk_count = group_width // chunk_width
+    rows = devices * tokens
+    total_blocks = rows // BLOCK
+    document = lax.axis_index("seq") // head_groups
+    own_lists = lax.dynamic_index_in_dim(random_blocks, document, 0, keepdims=False)
+    globals_here = lax.dynamic_index_in_dim(global_blocks, document, 0, keepdims=False)
+    positions = jnp.arange(total_blocks, dtype=jnp.int32)[:, None]
+    listed = jnp.concatenate(
+        [
+            jnp.broadcast_to(globals_here[None, :], (total_blocks, NGLOB)),
+            positions - 1,
+            positions,
+            positions + 1,
+            own_lists,
+        ],
+        axis=1,
+    )
+    listed = jnp.clip(listed, 0, total_blocks - 1)
+    chosen = (positions == globals_here[None, :]).astype(jnp.float32)
+    chosen = jnp.concatenate([chosen, 1.0 - jnp.sum(chosen, axis=1, keepdims=True)], axis=1)
+    blocked = (documents, tokens // BLOCK, BLOCK, features)
+    returned = pl.pallas_call(
+        functools.partial(fused_kernel, documents, chunk_count),
+        out_shape=jax.ShapeDtypeStruct(blocked, jnp.bfloat16),
+        in_specs=[pl.BlockSpec(memory_space=pltpu.SMEM)] * 3 + [pl.BlockSpec(memory_space=pl.ANY)] * 3,
+        out_specs=pl.BlockSpec(memory_space=pl.ANY),
+        scratch_shapes=[pltpu.VMEM((3, total_blocks, BLOCK, chunk_width), jnp.bfloat16)] * chunk_count
+        + [pltpu.VMEM((total_blocks, BLOCK, chunk_width), jnp.bfloat16)] * chunk_count
+        + [
+            pltpu.SemaphoreType.DMA((chunk_count,)),
+            pltpu.SemaphoreType.DMA((chunk_count,)),
+            pltpu.SemaphoreType.DMA((chunk_count,)),
+            pltpu.SemaphoreType.DMA,
+        ],
+        compiler_params=pltpu.CompilerParams(collective_id=0, has_side_effects=True),
+    )(
+        listed.reshape(-1).astype(jnp.int32),
+        globals_here.astype(jnp.int32),
+        chosen.reshape(-1),
+        queries.reshape(blocked),
+        key_states.reshape(blocked),
+        value_states.reshape(blocked),
+    )
+    return returned.reshape(queries.shape)
 
 
 def per_device(queries, key_states, value_states, random_blocks, global_blocks):
@@ -181,6 +382,14 @@
         P("groups", None, None),
         P("groups", None),
     )
+
+    def body(queries, *others):
+        heads = queries.shape[2] // HEAD_DIM
+        groups_needed = lax.axis_size("seq") // queries.shape[0]
+        if heads % (groups_needed * CHUNK_HEADS) == 0:
+            return per_device_fused(queries, *others)
+        return per_device(queries, *others)
+
     return jax.shard_map(
-        per_device, mesh=mesh, in_specs=placed, out_specs=P("groups", "seq", None), check_vma=False
-    )
+        body, mesh=mesh, in_specs=placed, out_specs=P("groups", "seq", None), check_vma=False
+    )

time: 261 us -> 193 us (0.74)
  Pallas kernels: 36.8 us -> 185 us
  waiting for transfers between devices: 106 us -> 0 us
  blocking collectives: 57.5 us -> 0 us
  starting transfers between devices: 29.3 us -> 0 us
  local copies, waits for them, and re-layouts: 29.4 us -> 5.39 us
    pallas_call x1, Pallas kernels: 36.8 us -> 185 us  [per_device_fused(): pl.pallas_call(functools.partial(fused_kernel, documents, chunk_count), o...]
    all_to_all x3 -> x0, waiting for transfers between devices: 106 us -> none  [the longest x1 39.3 us: per_device(): lax.all_to_all(by_parity(queries), 'seq', split_axis=0, concat_axis=1, ti...]
    all_to_all x1 -> x0, blocking collectives: 57.5 us -> none  [per_device(): lax.all_to_all(attended.reshape(devices, block_len, group_width), 'seq',...]
    all_to_all x3 -> x0, starting transfers between devices: 28.8 us -> none  [the longest x1 10.8 us: per_device(): lax.all_to_all(by_parity(queries), 'seq', split_axis=0, concat_axis=1, ti...]
    reshape x6 -> x1, local copies, waits for them, and re-layouts: 19.8 us -> 0.63 us  [per_device_fused(): chosen.reshape(-1)]
    transpose x3 -> x0, local copies, waits for them, and re-layouts: 9.06 us -> none  [by_parity(): pieces.transpose(0, 3, 1, 2, 4).reshape(devices, block_len, group_width)]
    unnamed x6, local copies, waits for them, and re-layouts: 0.01 us -> 3.14 us
  transfers between devices with their start and end apart: 5 -> 0, of which waited for: 3 -> 0; matrix products, arithmetic and copies ran while one was open for 7% -> 0% of each run, Pallas kernels for 0% -> 0%
where the time goes in v2:
time: 193 us; the launch traced here: 191 us
  Pallas kernels  185 us (96%)
  local copies, waits for them, and re-layouts  5.39 us (3%)
    pallas_call x1, Pallas kernels, per_device_fused(): pl.pallas_call(functools.partial(fused_kernel, documents, chunk_count), o...  185 us

profile of v2, /device:TPU:1, one launch (start us, length us, event | category | flops | bytes accessed | tf_op | source)
XLA Modules:
  0.0 190.5 jit_solution(1272624382810092363)
XLA Ops:
  0.0 0.0 copy-start
  0.0 0.7 dynamic-slice_bitcast_fusion.info
  0.7 0.0 copy-start.1
  0.7 0.1 fusion
  0.8 0.0 copy-done
  0.8 0.1 compare_convert_fusion
  0.9 0.1 broadcast_in_dim.5
  1.0 0.1 copy.7
  1.1 0.7 min.12.listed
  1.8 0.1 copy.8
  1.8 0.6 reshape.46.chosen
  2.5 0.0 copy-done.1
  2.5 184.9 %shard_map.55 = bf16[2,2,64,4096]{3,2,1,0:T(8,128)(2,1)} custom-call(s32[256]{0:T(256)} %min.12.listed, s32[2]{0:T(128)} %copy-done.1, f32[96]{0:T(128)} %reshape.46.chosen, bf16[2,2,64,4096]{3,2,1,0:T(8,128)(2,1)} %bitcast.12, bf16[2,2,64,4096]{3,2,1,0:T(8,128)(2,1)} %bitcast.13, bf16[2,2,64,4096]{3,2,1,0:T(8,128)(2,1)} %bitcast.14), custom_call_target="tpu_custom_call" | custom-call | tf_op jit(solution)/shard_map/pallas_call | solution.py:276
  187.4 3.1 %copy.13 = bf16[2,128,4096]{2,1,0:T(8,128)(2,1)} copy(bf16[2,128,4096]{2,1,0:T(8,128)(2,1)} %bitcast.11) | data formatting | bytes 4194304
  (8 shorter events, 0.1 us)
Async XLA Ops:
  0.0 0.8 copy-start
  0.7 1.8 copy-start.1

commit v3 on v2

--- a/solution.py
+++ b/solution.py
@@ -131,10 +131,19 @@
     lax.fori_loop(1, devices, greet, 0)
     pl.semaphore_wait(barrier, devices - 1)
 
+    half = devices // 2
+    side, seat = lax.div(me, half), lax.rem(me, half)
+
+    def far(step):
+        return (1 - side) * half + lax.rem(seat + step, half)
+
+    def near(step):
+        return side * half + lax.rem(seat + step, half)
+
     for chunk in range(chunk_count):
 
-        def send(step, carry):
-            target = lax.rem(me + step, devices)
+        def send(place, step, carry):
+            target = place(step)
             document, columns = outward(target, chunk)
             for which, source in enumerate(sources):
                 pltpu.make_async_remote_copy(
@@ -147,7 +156,8 @@
                 ).start()
             return carry
 
-        lax.fori_loop(1, devices, send, 0)
+        lax.fori_loop(0, half, functools.partial(send, far), 0)
+        lax.fori_loop(1, half, functools.partial(send, near), 0)
         document, columns = outward(me, chunk)
         for which, source in enumerate(sources):
             pltpu.make_async_copy(
@@ -214,8 +224,8 @@
     def give_back(chunk):
         document, columns = outward(me, chunk)
 
-        def send(step, carry):
-            target = lax.rem(me + step, devices)
+        def send(place, step, carry):
+            target = place(step)
             pltpu.make_async_remote_copy(
                 src_ref=made[chunk].at[blocks_of(target)],
                 dst_ref=out_hbm.at[document, :, :, columns],
@@ -226,7 +236,8 @@
             ).start()
             return carry
 
-        lax.fori_loop(1, devices, send, 0)
+        lax.fori_loop(0, half, functools.partial(send, far), 0)
+        lax.fori_loop(1, half, functools.partial(send, near), 0)
         pltpu.make_async_copy(made[chunk].at[blocks_of(me)], out_hbm.at[document, :, :, columns], back_recv_sem).start()
 
     for chunk in range(chunk_count):

time: 193 us -> 198 us (1.026); the launches traced: 191 us -> 198 us
  Pallas kernels: 185 us -> 192 us
    pallas_call x1, Pallas kernels: 185 us -> 192 us  [per_device_fused(): pl.pallas_call(functools.partial(fused_kernel, documents, chunk_count), o...]
where the time goes in v3:
time: 198 us
  Pallas kernels  192 us (97%)
  local copies, waits for them, and re-layouts  5.39 us (3%)
    pallas_call x1, Pallas kernels, per_device_fused(): pl.pallas_call(functools.partial(fused_kernel, documents, chunk_count), o...  192 us

profile of v3, /device:TPU:1, one launch (start us, length us, event | category | flops | bytes accessed | tf_op | source)
XLA Modules:
  0.0 197.6 jit_solution(11837091634924717135)
XLA Ops:
  0.0 0.0 copy-start
  0.0 0.7 dynamic-slice_bitcast_fusion.info
  0.7 0.0 copy-start.1
  0.7 0.1 fusion
  0.8 0.0 copy-done
  0.8 0.1 compare_convert_fusion
  0.9 0.1 broadcast_in_dim.5
  1.0 0.1 copy.7
  1.1 0.7 min.12.listed
  1.8 0.1 copy.8
  1.8 0.6 reshape.46.chosen
  2.5 0.0 copy-done.1
  2.5 192.0 %shard_map.55 = bf16[2,2,64,4096]{3,2,1,0:T(8,128)(2,1)} custom-call(s32[256]{0:T(256)} %min.12.listed, s32[2]{0:T(128)} %copy-done.1, f32[96]{0:T(128)} %reshape.46.chosen, bf16[2,2,64,4096]{3,2,1,0:T(8,128)(2,1)} %bitcast.12, bf16[2,2,64,4096]{3,2,1,0:T(8,128)(2,1)} %bitcast.13, bf16[2,2,64,4096]{3,2,1,0:T(8,128)(2,1)} %bitcast.14), custom_call_target="tpu_custom_call" | custom-call | tf_op jit(solution)/shard_map/pallas_call | solution.py:287
  194.5 3.1 %copy.13 = bf16[2,128,4096]{2,1,0:T(8,128)(2,1)} copy(bf16[2,128,4096]{2,1,0:T(8,128)(2,1)} %bitcast.11) | data formatting | bytes 4194304
  (8 shorter events, 0.1 us)
Async XLA Ops:
  0.0 0.8 copy-start
  0.7 1.8 copy-start.1
